TPU v7x, 256 devices: a whole 4x4x8 slice. The times are simulated.
256 devices in a mesh: blk: 256 (over y, z, x, core).
Axes of the slice: x: 4, y: 4, z: 8, core: 2. Of those that a mesh axis runs over, the one named last changes fastest.
Arguments:
- image_features: bfloat16 [65536, 1536], P('blk'), may hold values from -0.5 to 0.5
- head_weight: bfloat16 [1536, 1152], P('blk'), may hold values from -0.15625 to 0.15625
- text_embeds: bfloat16 [65536, 1152], P('blk'), may hold values from -0.29882812 to 0.29882812
- natural_exponent_factor: float32 [1], replicated, may hold values from 1.6 to 2.6
- logit_bias: float32 [1], replicated, may hold values from -4 to -1
Outputs:
- grad_features: bfloat16 [65536, 1536], P('blk')
- grad_text: bfloat16 [65536, 1152], P('blk')
- grad_weight: float32 [1536, 1152], P('blk')
All inputs are finite; a program needn't handle non-finite values.
Results may differ from a plain program's by a relative error of at most 0.0085.
Values may be sent and summed in bfloat16 or wider, within the bound.
No kernel may reach another device: no remote copies, remote signals or barrier semaphores. Data moves between devices by JAX's collectives and lax.ppermute only.
A program may use at most 64 MiB of HBM per device.

v0:
```python
import jax
import jax.numpy as jnp
from jax import lax
from jax.sharding import Mesh
from jax.sharding import PartitionSpec as P

S = 4
BLK = ("blk_0", "blk_1", "blk_2", "blk_3")
epsilon = 1e-06


def passed_along(block, axis, distance):
    devices = range(lax.axis_size(axis))
    route = [((i - distance) % len(devices), i) for i in devices]
    return lax.ppermute(block, axis, route)


def in_blocks(x, dim, peers):
    before, after = (x.shape[:dim], x.shape[dim + 1 :])
    return jnp.moveaxis(x.reshape(*before, peers, -1, *after), dim, 0)


def sent_and_summed(x, axis, dim):
    parts = in_blocks(x, dim, lax.axis_size(axis))
    arrived = lax.all_to_all(parts, axis, split_axis=0, concat_axis=0, tiled=True)
    return arrived.astype(jnp.float32).sum(axis=0)


def sum_by_axis(x, axes, dim):
    far, near = axes
    own = sent_and_summed(in_blocks(x, dim, lax.axis_size(far)), near, dim + 1)
    return jnp.sum(
        lax.all_to_all(own.astype(jnp.bfloat16), far, 0, 0, tiled=True).astype(jnp.float32), axis=0
    )


def normalize(rows):
    squares = jnp.sum(rows * rows, axis=1, keepdims=True)
    length = jnp.sqrt(squares + epsilon)
    return (rows / length, length)


def similarity_derivative(
    picture_sample_group,
    caption_sample_group,
    similarity_multiplier,
    neighbour_distance,
    outer_dimension_size,
):
    similarity_matrix = (
        similarity_multiplier
        * lax.dot_general(
            picture_sample_group,
            caption_sample_group,
            (((1,), (1,)), ((), ())),
            preferred_element_type=jnp.float32,
        )
        + neighbour_distance
    )
    if outer_dimension_size:
        matched = lax.broadcasted_iota(
            jnp.int32, similarity_matrix.shape, 0
        ) == lax.broadcasted_iota(jnp.int32, similarity_matrix.shape, 1)
        match_polarity = jnp.where(matched, 1.0, -1.0).astype(jnp.float32)
    else:
        match_polarity = -jnp.ones(similarity_matrix.shape, jnp.float32)
    return (
        -similarity_multiplier
        * match_polarity
        * jax.nn.sigmoid(-match_polarity * similarity_matrix)
    ).astype(jnp.bfloat16)


def project_back(grad, unit_rows, length):
    return (grad - unit_rows * jnp.sum(unit_rows * grad, axis=1, keepdims=True)) / length


def on_device(image_features, head_weight, text_embeds, natural_exponent_factor, logit_bias):
    full_weight = lax.all_gather(head_weight, BLK, axis=0, tiled=True)
    embedded = jnp.dot(image_features, full_weight, preferred_element_type=jnp.float32)
    image_unit, image_length = normalize(embedded)
    picture_embedding_mapped = image_unit.astype(jnp.bfloat16)
    text_unit, text_length = normalize(text_embeds.astype(jnp.float32))
    text_low = text_unit.astype(jnp.bfloat16)
    similarity_multiplier = jnp.exp(natural_exponent_factor[0])
    neighbour_distance = logit_bias[0]
    image_grad = jnp.zeros(image_unit.shape, jnp.float32)
    current_neighbour_tile = text_low
    for partition_portion in range(S):
        mapping_matrix = similarity_derivative(
            picture_embedding_mapped,
            current_neighbour_tile,
            similarity_multiplier,
            neighbour_distance,
            partition_portion == 0,
        )
        image_grad = image_grad + jnp.dot(
            mapping_matrix, current_neighbour_tile, preferred_element_type=jnp.float32
        )
        if partition_portion + 1 < S:
            current_neighbour_tile = passed_along(current_neighbour_tile, BLK, -1)
    text_grad = jnp.zeros(text_unit.shape, jnp.float32)
    passing = picture_embedding_mapped
    for partition_portion in range(S):
        mapping_matrix = similarity_derivative(
            passing, text_low, similarity_multiplier, neighbour_distance, partition_portion == 0
        )
        text_grad = text_grad + lax.dot_general(
            mapping_matrix, passing, (((0,), (0,)), ((), ())), preferred_element_type=jnp.float32
        )
        if partition_portion + 1 < S:
            passing = passed_along(passing, BLK, 1)
    embed_grad = project_back(image_grad, image_unit, image_length).astype(jnp.bfloat16)
    grad_text = project_back(text_grad, text_unit, text_length).astype(jnp.bfloat16)
    grad_features = lax.dot_general(
        embed_grad, full_weight, (((1,), (1,)), ((), ())), preferred_element_type=jnp.float32
    ).astype(jnp.bfloat16)
    grad_weight = sum_by_axis(
        lax.dot_general(
            image_features, embed_grad, (((0,), (0,)), ((), ())), preferred_element_type=jnp.float32
        ).astype(jnp.bfloat16),
        (("blk_0", "blk_1"), ("blk_2", "blk_3")),
        0,
    )
    return (grad_features, grad_text, grad_weight)


def solution(mesh):
    finer = Mesh(mesh.devices.reshape(4, 8, 4, 2), ("blk_0", "blk_1", "blk_2", "blk_3"))
    return jax.shard_map(
        on_device,
        mesh=finer,
        in_specs=(P(BLK, None), P(BLK, None), P(BLK, None), P(), P()),
        out_specs=(P(BLK, None), P(BLK, None), P(BLK, None)),
        check_vma=False,
    )
```

profile of v0, /device:TPU:37, one launch (start us, length us, event | category | flops | bytes accessed | tf_op | source)
XLA Modules:
  0.0 280.2 jit_solution(11349202122939430246)
XLA Ops:
  11.2 8.6 %collective-permute-done = bf16[256,1152]{1,0:T(8,128)(2,1)S(1)} collective-permute-done((bf16[256,1152]{1,0:T(8,128)(2,1)S(1)}, bf16[256,1152]{1,0:T(8,128)(2,1)S(1)}, u32[]{:S(2)}, u32[]{:S(2)}) %collective-permute-start) | collective-permute-done | bytes 589856 | tf_op jit(solution)/shard_map/ppermute | solution.py:15
  21.2 8.1 %collective-permute-done.1 = bf16[256,1152]{1,0:T(8,128)(2,1)} collective-permute-done((bf16[256,1152]{1,0:T(8,128)(2,1)S(1)}, bf16[256,1152]{1,0:T(8,128)(2,1)}, u32[]{:S(2)}, u32[]{:S(2)}) %collective-permute-start.1) | collective-permute-done | bytes 589856 | tf_op jit(solution)/shard_map/ppermute | solution.py:15
  29.3 100.3 %all-gather.3.cloned.1.call-done = bf16[256,6,1152]{2,1,0:T(8,128)(2,1)} async-done(((bf16[1,6,1152]{2,1,0:T(8,128)(2,1)}), bf16[256,6,1152]{2,1,0:T(8,128)(2,1)}) %all-gather.3.cloned.1.call-update) | async-done | bytes 3538960 | tf_op jit(solution)/shard_map/all_gather | solution.py:79
  129.6 6.8 %reshape.22 = bf16[1536,1152]{1,0:T(8,128)(2,1)} reshape(bf16[256,6,1152]{2,1,0:T(8,128)(2,1)} %all-gather.3.cloned.1.call-done) | data formatting | bytes 7077888
  136.4 3.3 %multiply_reduce_fusion.2 = (f32[256]{0:T(256)S(1)}, f32[256,1152]{1,0:T(8,128)S(1)}) fusion(bf16[256,1536]{1,0:T(8,128)(2,1)S(1)} %copy-done, bf16[1536,1152]{1,0:T(8,128)(2,1)} %reshape.22), kind=kOutput, calls=%fused_computation.17 | convolution fusion | flops 906559232 | bytes 5506048 | tf_op jit(solution)/shard_map/dot_general | solution.py:80
  142.2 2.6 convolution_add_fusion.5
  144.7 3.2 %convolution_add_fusion.4 = f32[256,1152]{1,0:T(8,128)} fusion(f32[256,1152]{1,0:T(8,128)S(1)} %convolution_add_fusion.5, bf16[256,1152]{1,0:T(8,128)(2,1)} %collective-permute-done.1, bf16[256,1152]{1,0:T(8,128)(2,1)S(1)} %fusion.83, f32[]{:T(128)S(6)} %mul.119, f32[]{:T(128)} %bitcast.39, f32[]{:T(128)} %bitcast), kind=kOutput, calls=%fused_computation.6 | convolution fusion | flops 302743552 | bytes 3538956 | tf_op jit(solution)/shard_map/dot_general | solution.py:97
  148.0 4.1 %multiply_reduce_fusion.1 = (f32[256]{0:T(256)S(1)}, f32[256,1152]{1,0:T(8,128)}) fusion(f32[256,1152]{1,0:T(8,128)} %copy-done.4, f32[256]{0:T(256)S(1)} %add_sqrt_fusion.1, f32[256,1152]{1,0:T(8,128)} %convolution_add_fusion.4, bf16[256,1152]{1,0:T(8,128)(2,1)} %collective-permute-done.2, bf16[256,1152]{1,0:T(8,128)(2,1)S(1)} %fusion.83, f32[]{:T(128)S(6)} %mul.119, ...), kind=kOutput, calls=%fused_computation.16 | convolution fusion | flops 303628032 | bytes 4720652 | tf_op jit(solution)/shard_map/dot_general | solution.py:97
  152.0 4.3 %fusion = bf16[1536,1152]{0,1:T(8,128)(2,1)} fusion(bf16[256,1536]{1,0:T(8,128)(2,1)S(1)} %copy-done, f32[256,1152]{1,0:T(8,128)} %get-tuple-element.6, f32[256]{0:T(256)S(1)} %get-tuple-element.5, f32[256]{0:T(256)S(1)} %add_sqrt_fusion.1, f32[256,1152]{1,0:T(8,128)S(1)} %copy-done.5), kind=kOutput, calls=%fused_computation.1 | convolution fusion | flops 909213696 | bytes 6686720 | tf_op jit(solution)/shard_map/dot_general | solution.py:119
  156.3 5.8 %copy.13 = bf16[1536,1152]{1,0:T(8,128)(2,1)} copy(bf16[1536,1152]{0,1:T(8,128)(2,1)} %fusion) | data formatting | bytes 7077888 | tf_op jit(solution)/shard_map/convert_element_type | solution.py:121
  162.2 6.7 %reshape_reshape.3 = bf16[32,8,6,1152]{3,2,1,0:T(8,128)(2,1)} reshape(bf16[1536,1152]{1,0:T(8,128)(2,1)} %copy.13) | data formatting | bytes 7077888 | tf_op jit(solution)/shard_map/reshape;reshape | solution.py:20
  168.8 6.2 %copy.14 = bf16[8,32,6,1152]{3,1,2,0:T(8,128)(2,1)} copy(bf16[8,32,6,1152]{3,2,0,1:T(8,128)(2,1)} %bitcast.41) | data formatting | bytes 7077888 | tf_op jit(solution)/shard_map/transpose | solution.py:20
  175.0 4.9 %all-to-all-start = ((bf16[8,32,6,1152]{3,1,2,0:T(8,128)(2,1)}), bf16[8,32,6,1152]{3,1,2,0:T(8,128)(2,1)}, u32[]{:S(2)}, u32[]{:S(2)}) async-start(bf16[8,32,6,1152]{3,1,2,0:T(8,128)(2,1)} %copy.14), calls=%async_computation | async-start | bytes 7077888 | tf_op jit(solution)/shard_map/all_to_all | solution.py:25
  182.4 42.4 %collective-permute-done.3 = bf16[256,1152]{1,0:T(8,128)(2,1)S(1)} collective-permute-done((bf16[256,1152]{1,0:T(8,128)(2,1)S(1)}, bf16[256,1152]{1,0:T(8,128)(2,1)S(1)}, u32[]{:S(2)}, u32[]{:S(2)}) %collective-permute-start.3) | collective-permute-done | bytes 589856 | tf_op jit(solution)/shard_map/ppermute | solution.py:15
  224.8 2.5 collective-permute-start.4
  227.3 4.5 %convolution_convert_fusion.1 = bf16[256,1536]{1,0:T(8,128)(2,1)} fusion(bf16[1536,1152]{1,0:T(8,128)(2,1)} %reshape.22, f32[256,1152]{1,0:T(8,128)} %get-tuple-element.6, f32[256]{0:T(256)S(1)} %get-tuple-element.5, f32[256]{0:T(256)S(1)} %add_sqrt_fusion.1, f32[256,1152]{1,0:T(8,128)S(1)} %copy-done.6), kind=kOutput, calls=%fused_computation.8 | convolution fusion | flops 907837440 | bytes 6686720 | tf_op jit(solution)/shard_map/dot_general | solution.py:115
  231.8 2.3 collective-permute-done.4
  234.1 2.5 collective-permute-start.5
  236.6 2.7 convolution_add_fusion.2
  241.3 2.5 reduce_sum.61
  244.9 9.5 %all-to-all-start.1 = ((bf16[32,6,1152]{2,1,0:T(8,128)(2,1)}), bf16[32,6,1152]{2,1,0:T(8,128)(2,1)S(1)}, u32[]{:S(2)}, u32[]{:S(2)}) async-start(bf16[32,6,1152]{2,1,0:T(8,128)(2,1)} %copy.15), calls=%async_computation.1 | async-start | bytes 1179648 | tf_op jit(solution)/shard_map/all_to_all | solution.py:33
  254.4 3.7 %multiply_reduce_fusion = (f32[256]{0:T(256)S(1)}, f32[256,1152]{1,0:T(8,128)}) fusion(f32[256]{0:T(256)S(1)} %add_sqrt_fusion, bf16[256,1152]{1,0:T(8,128)(2,1)S(1)} %copy-done.1, f32[256,1152]{1,0:T(8,128)} %convolution_add_fusion.1, bf16[256,1152]{1,0:T(8,128)(2,1)} %collective-permute-done.5, bf16[256,1152]{1,0:T(8,128)(2,1)S(1)} %fusion.82, ...), kind=kOutput, calls=%fused_computation.14 | convolution fusion | flops 303922944 | bytes 4130828 | tf_op jit(solution)/shard_map/dot_general | solution.py:108
  258.1 2.4 divide_convert_fusion
  260.5 12.2 %all-to-all-done.1 = bf16[32,6,1152]{2,1,0:T(8,128)(2,1)S(1)} async-done(((bf16[32,6,1152]{2,1,0:T(8,128)(2,1)}), bf16[32,6,1152]{2,1,0:T(8,128)(2,1)S(1)}, u32[]{:S(2)}, u32[]{:S(2)}) %all-to-all-start.1) | async-done | bytes 442400 | tf_op jit(solution)/shard_map/all_to_all | solution.py:33
  (34 shorter events, 12.9 us)
Async XLA Ops:
  7.2 129.2 %copy-start = (bf16[256,1536]{1,0:T(8,128)(2,1)S(1)}, bf16[256,1536]{1,0:T(8,128)(2,1)}, u32[]{:S(2)}) copy-start(bf16[256,1536]{1,0:T(8,128)(2,1)} %param.5) | copy-start | bytes 2359300
  7.2 122.4 %all-gather.3.cloned.1.call-start = ((), (), s32[]{:S(2)}) async-start(), calls=%async_computation.2 | async-start | bytes 4737024 | tf_op jit(solution)/shard_map/all_gather | solution.py:79
  10.5 9.4 %collective-permute-start = (bf16[256,1152]{1,0:T(8,128)(2,1)S(1)}, bf16[256,1152]{1,0:T(8,128)(2,1)S(1)}, u32[]{:S(2)}, u32[]{:S(2)}) collective-permute-start(bf16[256,1152]{1,0:T(8,128)(2,1)S(1)} %fusion.82), channel_id=1, source_target_pairs={{1,0},{2,1},{3,2},{4,3},{5,4},{6,5},{7,6},{8,7},{9,8},{10,9},{11,1... | collective-permute-start | bytes 1769480 | tf_op jit(solution)/shard_map/ppermute | solution.py:15
  19.9 116.5 %copy-start.2 = (bf16[256,1152]{1,0:T(8,128)(2,1)}, bf16[256,1152]{1,0:T(8,128)(2,1)S(1)}, u32[]{:S(2)}) copy-start(bf16[256,1152]{1,0:T(8,128)(2,1)S(1)} %collective-permute-done) | copy-start | bytes 1769476
  19.9 9.4 %collective-permute-start.1 = (bf16[256,1152]{1,0:T(8,128)(2,1)S(1)}, bf16[256,1152]{1,0:T(8,128)(2,1)}, u32[]{:S(2)}, u32[]{:S(2)}) collective-permute-start(bf16[256,1152]{1,0:T(8,128)(2,1)S(1)} %collective-permute-done), channel_id=1, source_target_pairs={{1,0},{2,1},{3,2},{4,3},{5,4},{6,5},{7,6},{8,7},{9,8},{10,9},{11,1... | collective-permute-start | bytes 1769480 | tf_op jit(solution)/shard_map/ppermute | solution.py:15
  29.3 118.7 %collective-permute-start.2 = (bf16[256,1152]{1,0:T(8,128)(2,1)}, bf16[256,1152]{1,0:T(8,128)(2,1)}, u32[]{:S(2)}, u32[]{:S(2)}) collective-permute-start(bf16[256,1152]{1,0:T(8,128)(2,1)} %collective-permute-done.1), channel_id=1, source_target_pairs={{1,0},{2,1},{3,2},{4,3},{5,4},{6,5},{7,6},{8,7},{9,8},{10,9},{11,1... | collective-permute-start | bytes 1769480 | tf_op jit(solution)/shard_map/ppermute | solution.py:15
  139.7 1.1 copy-start.4
  148.0 4.1 %copy-start.5 = (f32[256,1152]{1,0:T(8,128)S(1)}, f32[256,1152]{1,0:T(8,128)}, u32[]{:S(2)}) copy-start(f32[256,1152]{1,0:T(8,128)} %copy-done.4) | copy-start | bytes 3538948
  175.0 66.3 %all-to-all-start = ((bf16[8,32,6,1152]{3,1,2,0:T(8,128)(2,1)}), bf16[8,32,6,1152]{3,1,2,0:T(8,128)(2,1)}, u32[]{:S(2)}, u32[]{:S(2)}) async-start(bf16[8,32,6,1152]{3,1,2,0:T(8,128)(2,1)} %copy.14), calls=%async_computation | async-start | bytes 7077888 | tf_op jit(solution)/shard_map/all_to_all | solution.py:25
  179.9 47.4 %copy-start.6 = (f32[256,1152]{1,0:T(8,128)S(1)}, f32[256,1152]{1,0:T(8,128)}, u32[]{:S(2)}) copy-start(f32[256,1152]{1,0:T(8,128)} %copy-done.4) | copy-start | bytes 3538948
  179.9 45.0 %collective-permute-start.3 = (bf16[256,1152]{1,0:T(8,128)(2,1)S(1)}, bf16[256,1152]{1,0:T(8,128)(2,1)S(1)}, u32[]{:S(2)}, u32[]{:S(2)}) collective-permute-start(bf16[256,1152]{1,0:T(8,128)(2,1)S(1)} %fusion.83), channel_id=1, source_target_pairs={{255,0},{0,1},{1,2},{2,3},{3,4},{4,5},{5,6},{6,7},{7,8},{8,9},{9,1... | collective-permute-start | bytes 1769480 | tf_op jit(solution)/shard_map/ppermute | solution.py:15
  224.8 7.0 %copy-start.3 = (bf16[256,1152]{1,0:T(8,128)(2,1)}, bf16[256,1152]{1,0:T(8,128)(2,1)S(1)}, u32[]{:S(2)}) copy-start(bf16[256,1152]{1,0:T(8,128)(2,1)S(1)} %collective-permute-done.3) | copy-start | bytes 1769476
  224.8 9.3 %collective-permute-start.4 = (bf16[256,1152]{1,0:T(8,128)(2,1)S(1)}, bf16[256,1152]{1,0:T(8,128)(2,1)S(1)}, u32[]{:S(2)}, u32[]{:S(2)}) collective-permute-start(bf16[256,1152]{1,0:T(8,128)(2,1)S(1)} %collective-permute-done.3), channel_id=1, source_target_pairs={{255,0},{0,1},{1,2},{2,3},{3,4},{4,5},{5,6},{6,7},{7,8},{8,9},{9,1... | collective-permute-start | bytes 1769480 | tf_op jit(solution)/shard_map/ppermute | solution.py:15
  234.1 20.2 %collective-permute-start.5 = (bf16[256,1152]{1,0:T(8,128)(2,1)S(1)}, bf16[256,1152]{1,0:T(8,128)(2,1)}, u32[]{:S(2)}, u32[]{:S(2)}) collective-permute-start(bf16[256,1152]{1,0:T(8,128)(2,1)S(1)} %collective-permute-done.4), channel_id=1, source_target_pairs={{255,0},{0,1},{1,2},{2,3},{3,4},{4,5},{5,6},{6,7},{7,8},{8,9},{9,1... | collective-permute-start | bytes 1769480 | tf_op jit(solution)/shard_map/ppermute | solution.py:15
  243.9 10.5 %copy-start.1 = (bf16[256,1152]{1,0:T(8,128)(2,1)S(1)}, bf16[256,1152]{1,0:T(8,128)(2,1)}, u32[]{:S(2)}) copy-start(bf16[256,1152]{1,0:T(8,128)(2,1)} %param.7) | copy-start | bytes 1769476
  244.9 27.8 %all-to-all-start.1 = ((bf16[32,6,1152]{2,1,0:T(8,128)(2,1)}), bf16[32,6,1152]{2,1,0:T(8,128)(2,1)S(1)}, u32[]{:S(2)}, u32[]{:S(2)}) async-start(bf16[32,6,1152]{2,1,0:T(8,128)(2,1)} %copy.15), calls=%async_computation.1 | async-start | bytes 1179648 | tf_op jit(solution)/shard_map/all_to_all | solution.py:33
Sparse Core Ops, SparseCore 0:
  11.8 117.7 all-gather.2
where the time goes:
time: 281 us; the launch traced here: 280 us
  waiting for transfers between devices  175 us (62%)
  matrix products  33.6 us (12%)
  local copies, waits for them, and re-layouts  26.9 us (10%)
  starting transfers between devices  21.3 us (8%)
  between operations  15.5 us (6%)
  other arithmetic  8.36 us (3%)
    all_gather x1, waiting for transfers between devices, on_device(): full_weight = lax.all_gather(head_weight, BLK, axis=0, tiled=True)  100 us
    ppermute x6, waiting for transfers between devices, passed_along(): return lax.ppermute(block, axis, route)  61.4 us
    all_to_all x1, waiting for transfers between devices, sum_by_axis(): lax.all_to_all(own.astype(jnp.bfloat16), far, 0, 0, tiled=True)  12.2 us
    dot_general x4, matrix products, on_device(): jnp.dot(mapping_matrix, current_neighbour_tile, preferred_element_type=jn...  11.3 us
    dot_general x4, matrix products, on_device(): lax.dot_general(mapping_matrix, passing, (((0,), (0,)), ((), ())), prefer...  9.82 us
    all_to_all x1, starting transfers between devices, sum_by_axis(): lax.all_to_all(own.astype(jnp.bfloat16), far, 0, 0, tiled=True)  9.49 us
    unnamed x15, local copies, waits for them, and re-layouts  7.29 us
    ppermute x6, starting transfers between devices, passed_along(): return lax.ppermute(block, axis, route)  6.89 us
  transfers between devices with their start and end apart: 9, of which 6 were waited for; matrix products, arithmetic and copies ran while one was open for 14% of the time, Pallas kernels for 0%

commit v1 on v0

--- a/solution.py
+++ b/solution.py
@@ -76,7 +76,9 @@
 
 
 def on_device(image_features, head_weight, text_embeds, natural_exponent_factor, logit_bias):
-    full_weight = lax.all_gather(head_weight, BLK, axis=0, tiled=True)
+    full_weight = jnp.concatenate(
+        lax.all_to_all(jnp.stack([head_weight] * lax.axis_size(BLK)), BLK, 0, 0), axis=0
+    )
     embedded = jnp.dot(image_features, full_weight, preferred_element_type=jnp.float32)
     image_unit, image_length = normalize(embedded)
     picture_embedding_mapped = image_unit.astype(jnp.bfloat16)

time: 281 us -> 293 us (1.043)
  starting transfers between devices: 21.3 us -> 54.5 us
  between operations: 15.5 us -> 2.07 us
  waiting for transfers between devices: 175 us -> 162 us
  local copies, waits for them, and re-layouts: 26.9 us -> 30.1 us
  matrix products: 33.6 us -> 36.8 us
    all_gather x1 -> x0, waiting for transfers between devices: 100 us -> none  [on_device(): full_weight = lax.all_gather(head_weight, BLK, axis=0, tiled=True)]
    all_to_all x0 -> x1, waiting for transfers between devices: none -> 68.7 us  [on_device(): lax.all_to_all(jnp.stack([head_weight] * lax.axis_size(BLK)), BLK, 0, 0)]
    ppermute x6, waiting for transfers between devices: 61.4 us -> 81.6 us  [passed_along(): return lax.ppermute(block, axis, route)]
    all_to_all x1, starting transfers between devices: 4.86 us -> 20.6 us  [sent_and_summed(): lax.all_to_all(parts, axis, split_axis=0, concat_axis=0, tiled=True)]
    all_to_all x0 -> x1, starting transfers between devices: none -> 15.5 us  [on_device(): lax.all_to_all(jnp.stack([head_weight] * lax.axis_size(BLK)), BLK, 0, 0)]
    unnamed x15 -> x8, local copies, waits for them, and re-layouts: 7.29 us -> 0.49 us
    reshape x0 -> x1, local copies, waits for them, and re-layouts: none -> 6.77 us  [on_device(): jnp.concatenate(lax.all_to_all(jnp.stack([head_weight] * lax.axis_size(BL...]
    another operation x0 -> x1, local copies, waits for them, and re-layouts: none -> 3.29 us  [on_device(): jnp.stack([head_weight] * lax.axis_size(BLK))]
where the time goes in v1:
time: 293 us; the launch traced here: 292 us
  waiting for transfers between devices  162 us (55%)
  starting transfers between devices  54.5 us (19%)
  matrix products  36.8 us (13%)
  local copies, waits for them, and re-layouts  30.1 us (10%)
  other arithmetic  6.24 us (2%)
    ppermute x6, waiting for transfers between devices, passed_along(): return lax.ppermute(block, axis, route)  81.6 us
    all_to_all x1, waiting for transfers between devices, on_device(): lax.all_to_all(jnp.stack([head_weight] * lax.axis_size(BLK)), BLK, 0, 0)  68.7 us
    all_to_all x1, starting transfers between devices, sent_and_summed(): lax.all_to_all(parts, axis, split_axis=0, concat_axis=0, tiled=True)  20.6 us
    all_to_all x1, starting transfers between devices, on_device(): lax.all_to_all(jnp.stack([head_weight] * lax.axis_size(BLK)), BLK, 0, 0)  15.5 us
    dot_general x4, matrix products, on_device(): jnp.dot(mapping_matrix, current_neighbour_tile, preferred_element_type=jn...  12.3 us
    all_to_all x1, waiting for transfers between devices, sum_by_axis(): lax.all_to_all(own.astype(jnp.bfloat16), far, 0, 0, tiled=True)  12.2 us
    all_to_all x1, starting transfers between devices, sum_by_axis(): lax.all_to_all(own.astype(jnp.bfloat16), far, 0, 0, tiled=True)  11.8 us
    dot_general x4, matrix products, on_device(): lax.dot_general(mapping_matrix, passing, (((0,), (0,)), ((), ())), prefer...  11.7 us
  transfers between devices with their start and end apart: 9, of which 6 were waited for; matrix products, arithmetic and copies ran while one was open for 14% of the time, Pallas kernels for 0%

profile of v1, /device:TPU:37, one launch (start us, length us, event | category | flops | bytes accessed | tf_op | source)
XLA Modules:
  0.0 292.1 jit_solution(4390223563263706028)
XLA Ops:
  0.6 3.3 %stack.2 = bf16[256,6,1152]{2,1,0:T(8,128)(2,1)} broadcast(bf16[6,1152]{1,0:T(8,128)(2,1)} %param.6), dimensions={1,2} | broadcast | bytes 3552768 | tf_op jit(solution)/shard_map/stack | solution.py:80
  3.9 15.5 %all-to-all-start = ((bf16[256,6,1152]{2,1,0:T(8,128)(2,1)}), bf16[256,6,1152]{2,1,0:T(8,128)(2,1)}, u32[]{:S(2)}, u32[]{:S(2)}) async-start(bf16[256,6,1152]{2,1,0:T(8,128)(2,1)} %stack.2), calls=%async_computation | async-start | bytes 9437184 | tf_op jit(solution)/shard_map/all_to_all | solution.py:80
  20.4 21.6 %collective-permute-done = bf16[256,1152]{1,0:T(8,128)(2,1)S(1)} collective-permute-done((bf16[256,1152]{1,0:T(8,128)(2,1)S(1)}, bf16[256,1152]{1,0:T(8,128)(2,1)S(1)}, u32[]{:S(2)}, u32[]{:S(2)}) %collective-permute-start) | collective-permute-done | bytes 589856 | tf_op jit(solution)/shard_map/ppermute | solution.py:15
  43.3 13.9 %collective-permute-done.1 = bf16[256,1152]{1,0:T(8,128)(2,1)} collective-permute-done((bf16[256,1152]{1,0:T(8,128)(2,1)S(1)}, bf16[256,1152]{1,0:T(8,128)(2,1)}, u32[]{:S(2)}, u32[]{:S(2)}) %collective-permute-start.1) | collective-permute-done | bytes 589856 | tf_op jit(solution)/shard_map/ppermute | solution.py:15
  57.2 68.7 %all-to-all-done = bf16[256,6,1152]{2,1,0:T(8,128)(2,1)} async-done(((bf16[256,6,1152]{2,1,0:T(8,128)(2,1)}), bf16[256,6,1152]{2,1,0:T(8,128)(2,1)}, u32[]{:S(2)}, u32[]{:S(2)}) %all-to-all-start) | async-done | bytes 3538976 | tf_op jit(solution)/shard_map/all_to_all | solution.py:80
  125.9 6.8 %reshape.26 = bf16[1536,1152]{1,0:T(8,128)(2,1)} reshape(bf16[256,6,1152]{2,1,0:T(8,128)(2,1)} %all-to-all-done) | data formatting | bytes 7077888 | tf_op jit(solution)/shard_map/reshape | solution.py:79
  132.7 3.3 %multiply_reduce_fusion.2 = (f32[256]{0:T(256)S(1)}, f32[256,1152]{1,0:T(8,128)S(1)}) fusion(bf16[256,1536]{1,0:T(8,128)(2,1)S(1)} %copy-done, bf16[1536,1152]{1,0:T(8,128)(2,1)} %reshape.26), kind=kOutput, calls=%fused_computation.17 | convolution fusion | flops 906559232 | bytes 5506048 | tf_op jit(solution)/shard_map/dot_general | solution.py:82
  138.4 3.3 %convolution_add_fusion.5 = f32[256,1152]{1,0:T(8,128)} fusion(f32[256,1152]{1,0:T(8,128)} %fusion.84, bf16[256,1152]{1,0:T(8,128)(2,1)S(1)} %collective-permute-done, bf16[256,1152]{1,0:T(8,128)(2,1)S(1)} %fusion.83, f32[]{:T(128)S(6)} %mul.119, f32[]{:T(128)} %bitcast.39, f32[]{:T(128)} %bitcast), kind=kOutput, calls=%fused_computation.7 | convolution fusion | flops 302743552 | bytes 3538956 | tf_op jit(solution)/shard_map/dot_general | solution.py:99
  141.7 3.6 %convolution_add_fusion.4 = f32[256,1152]{1,0:T(8,128)} fusion(f32[256,1152]{1,0:T(8,128)} %convolution_add_fusion.5, bf16[256,1152]{1,0:T(8,128)(2,1)} %collective-permute-done.1, bf16[256,1152]{1,0:T(8,128)(2,1)S(1)} %fusion.83, f32[]{:T(128)S(6)} %mul.119, f32[]{:T(128)} %bitcast.38, f32[]{:T(128)} %bitcast), kind=kOutput, calls=%fused_computation.6 | convolution fusion | flops 302743552 | bytes 3538956 | tf_op jit(solution)/shard_map/dot_general | solution.py:99
  145.3 4.0 %multiply_reduce_fusion.1 = (f32[256]{0:T(256)S(1)}, f32[256,1152]{1,0:T(8,128)}) fusion(f32[256,1152]{1,0:T(8,128)} %copy-done.2, f32[256]{0:T(256)S(1)} %add_sqrt_fusion.1, f32[256,1152]{1,0:T(8,128)} %convolution_add_fusion.4, bf16[256,1152]{1,0:T(8,128)(2,1)} %collective-permute-done.2, bf16[256,1152]{1,0:T(8,128)(2,1)S(1)} %fusion.83, f32[]{:T(128)S(6)} %mul.119, ...), kind=kOutput, calls=%fused_computation.16 | convolution fusion | flops 303628032 | bytes 4720652 | tf_op jit(solution)/shard_map/dot_general | solution.py:99
  149.3 4.7 %fusion = bf16[1536,1152]{0,1:T(8,128)(2,1)} fusion(bf16[256,1536]{1,0:T(8,128)(2,1)S(1)} %copy-done, f32[256,1152]{1,0:T(8,128)} %get-tuple-element.6, f32[256]{0:T(256)S(1)} %get-tuple-element.5, f32[256]{0:T(256)S(1)} %add_sqrt_fusion.1, f32[256,1152]{1,0:T(8,128)} %copy-done.2), kind=kOutput, calls=%fused_computation.1 | convolution fusion | flops 909213696 | bytes 6686720 | tf_op jit(solution)/shard_map/dot_general | solution.py:121
  153.9 5.8 %copy.13 = bf16[1536,1152]{1,0:T(8,128)(2,1)} copy(bf16[1536,1152]{0,1:T(8,128)(2,1)} %fusion) | data formatting | bytes 7077888 | tf_op jit(solution)/shard_map/convert_element_type | solution.py:123
  159.7 6.7 %reshape_reshape.3 = bf16[32,8,6,1152]{3,2,1,0:T(8,128)(2,1)} reshape(bf16[1536,1152]{1,0:T(8,128)(2,1)} %copy.13) | data formatting | bytes 7077888 | tf_op jit(solution)/shard_map/reshape;reshape | solution.py:20
  166.4 6.2 %copy.14 = bf16[8,32,6,1152]{3,1,2,0:T(8,128)(2,1)} copy(bf16[8,32,6,1152]{3,2,0,1:T(8,128)(2,1)} %bitcast.40) | data formatting | bytes 7077888 | tf_op jit(solution)/shard_map/transpose | solution.py:20
  172.6 20.6 %all-to-all-start.1 = ((bf16[8,32,6,1152]{3,1,2,0:T(8,128)(2,1)}), bf16[8,32,6,1152]{3,1,2,0:T(8,128)(2,1)}, u32[]{:S(2)}, u32[]{:S(2)}) async-start(bf16[8,32,6,1152]{3,1,2,0:T(8,128)(2,1)} %copy.14), calls=%async_computation.1 | async-start | bytes 7077888 | tf_op jit(solution)/shard_map/all_to_all | solution.py:25
  195.7 43.7 %collective-permute-done.3 = bf16[256,1152]{1,0:T(8,128)(2,1)S(1)} collective-permute-done((bf16[256,1152]{1,0:T(8,128)(2,1)S(1)}, bf16[256,1152]{1,0:T(8,128)(2,1)S(1)}, u32[]{:S(2)}, u32[]{:S(2)}) %collective-permute-start.3) | collective-permute-done | bytes 589856 | tf_op jit(solution)/shard_map/ppermute | solution.py:15
  239.5 2.5 collective-permute-start.4
  241.9 4.5 %convolution_convert_fusion.1 = bf16[256,1536]{1,0:T(8,128)(2,1)} fusion(bf16[1536,1152]{1,0:T(8,128)(2,1)} %reshape.26, f32[256,1152]{1,0:T(8,128)} %get-tuple-element.6, f32[256]{0:T(256)S(1)} %get-tuple-element.5, f32[256]{0:T(256)S(1)} %add_sqrt_fusion.1, f32[256,1152]{1,0:T(8,128)S(1)} %copy-done.3), kind=kOutput, calls=%fused_computation.8 | convolution fusion | flops 907837440 | bytes 6686720 | tf_op jit(solution)/shard_map/dot_general | solution.py:117
  251.2 3.3 %convolution_add_fusion.2 = f32[256,1152]{1,0:T(8,128)} fusion(f32[256,1152]{1,0:T(8,128)} %fusion.85, bf16[256,1152]{1,0:T(8,128)(2,1)S(1)} %collective-permute-done.3, bf16[256,1152]{1,0:T(8,128)(2,1)S(1)} %fusion.82, f32[]{:T(128)S(6)} %mul.119, f32[]{:T(128)} %bitcast.36, f32[]{:T(128)} %bitcast), kind=kOutput, calls=%fused_computation.4 | convolution fusion | flops 302743552 | bytes 3538956 | tf_op jit(solution)/shard_map/dot_general | solution.py:110
  254.6 3.3 %convolution_add_fusion.1 = f32[256,1152]{1,0:T(8,128)} fusion(f32[256,1152]{1,0:T(8,128)} %convolution_add_fusion.2, bf16[256,1152]{1,0:T(8,128)(2,1)S(1)} %collective-permute-done.4, bf16[256,1152]{1,0:T(8,128)(2,1)S(1)} %fusion.82, f32[]{:T(128)S(6)} %mul.119, f32[]{:T(128)} %bitcast.35, f32[]{:T(128)} %bitcast), kind=kOutput, calls=%fused_computation.3 | convolution fusion | flops 302743552 | bytes 3538956 | tf_op jit(solution)/shard_map/dot_general | solution.py:110
  257.9 2.5 reduce_sum.61
  261.4 11.8 %all-to-all-start.2 = ((bf16[32,6,1152]{2,1,0:T(8,128)(2,1)}), bf16[32,6,1152]{2,1,0:T(8,128)(2,1)S(1)}, u32[]{:S(2)}, u32[]{:S(2)}) async-start(bf16[32,6,1152]{2,1,0:T(8,128)(2,1)} %copy.15), calls=%async_computation.2 | async-start | bytes 1179648 | tf_op jit(solution)/shard_map/all_to_all | solution.py:33
  273.1 3.7 %multiply_reduce_fusion = (f32[256]{0:T(256)S(1)}, f32[256,1152]{1,0:T(8,128)}) fusion(f32[256]{0:T(256)S(1)} %add_sqrt_fusion, bf16[256,1152]{1,0:T(8,128)(2,1)S(1)} %copy-done.1, f32[256,1152]{1,0:T(8,128)} %convolution_add_fusion.1, bf16[256,1152]{1,0:T(8,128)(2,1)} %collective-permute-done.5, bf16[256,1152]{1,0:T(8,128)(2,1)S(1)} %fusion.82, ...), kind=kOutput, calls=%fused_computation.14 | convolution fusion | flops 303922944 | bytes 4130828 | tf_op jit(solution)/shard_map/dot_general | solution.py:110
  279.2 12.2 %all-to-all-done.2 = bf16[32,6,1152]{2,1,0:T(8,128)(2,1)S(1)} async-done(((bf16[32,6,1152]{2,1,0:T(8,128)(2,1)}), bf16[32,6,1152]{2,1,0:T(8,128)(2,1)S(1)}, u32[]{:S(2)}, u32[]{:S(2)}) %all-to-all-start.2) | async-done | bytes 442400 | tf_op jit(solution)/shard_map/all_to_all | solution.py:33
  (28 shorter events, 14.8 us)
Async XLA Ops:
  0.6 132.0 %copy-start = (bf16[256,1536]{1,0:T(8,128)(2,1)S(1)}, bf16[256,1536]{1,0:T(8,128)(2,1)}, u32[]{:S(2)}) copy-start(bf16[256,1536]{1,0:T(8,128)(2,1)} %param.5) | copy-start | bytes 2359300
  3.9 15.5 %copy-start.1 = (bf16[256,1152]{1,0:T(8,128)(2,1)S(1)}, bf16[256,1152]{1,0:T(8,128)(2,1)}, u32[]{:S(2)}) copy-start(bf16[256,1152]{1,0:T(8,128)(2,1)} %param.7) | copy-start | bytes 1769476
  3.9 122.0 %all-to-all-start = ((bf16[256,6,1152]{2,1,0:T(8,128)(2,1)}), bf16[256,6,1152]{2,1,0:T(8,128)(2,1)}, u32[]{:S(2)}, u32[]{:S(2)}) async-start(bf16[256,6,1152]{2,1,0:T(8,128)(2,1)} %stack.2), calls=%async_computation | async-start | bytes 9437184 | tf_op jit(solution)/shard_map/all_to_all | solution.py:80
  19.9 22.0 %collective-permute-start = (bf16[256,1152]{1,0:T(8,128)(2,1)S(1)}, bf16[256,1152]{1,0:T(8,128)(2,1)S(1)}, u32[]{:S(2)}, u32[]{:S(2)}) collective-permute-start(bf16[256,1152]{1,0:T(8,128)(2,1)S(1)} %fusion.82), channel_id=1, source_target_pairs={{1,0},{2,1},{3,2},{4,3},{5,4},{6,5},{7,6},{8,7},{9,8},{10,9},{11,1... | collective-permute-start | bytes 1769480 | tf_op jit(solution)/shard_map/ppermute | solution.py:15
  42.0 15.2 %collective-permute-start.1 = (bf16[256,1152]{1,0:T(8,128)(2,1)S(1)}, bf16[256,1152]{1,0:T(8,128)(2,1)}, u32[]{:S(2)}, u32[]{:S(2)}) collective-permute-start(bf16[256,1152]{1,0:T(8,128)(2,1)S(1)} %collective-permute-done), channel_id=1, source_target_pairs={{1,0},{2,1},{3,2},{4,3},{5,4},{6,5},{7,6},{8,7},{9,8},{10,9},{11,1... | collective-permute-start | bytes 1769480 | tf_op jit(solution)/shard_map/ppermute | solution.py:15
  57.2 88.1 %collective-permute-start.2 = (bf16[256,1152]{1,0:T(8,128)(2,1)}, bf16[256,1152]{1,0:T(8,128)(2,1)}, u32[]{:S(2)}, u32[]{:S(2)}) collective-permute-start(bf16[256,1152]{1,0:T(8,128)(2,1)} %collective-permute-done.1), channel_id=1, source_target_pairs={{1,0},{2,1},{3,2},{4,3},{5,4},{6,5},{7,6},{8,7},{9,8},{10,9},{11,1... | collective-permute-start | bytes 1769480 | tf_op jit(solution)/shard_map/ppermute | solution.py:15
  135.9 1.1 copy-start.2
  172.6 85.3 %all-to-all-start.1 = ((bf16[8,32,6,1152]{3,1,2,0:T(8,128)(2,1)}), bf16[8,32,6,1152]{3,1,2,0:T(8,128)(2,1)}, u32[]{:S(2)}, u32[]{:S(2)}) async-start(bf16[8,32,6,1152]{3,1,2,0:T(8,128)(2,1)} %copy.14), calls=%async_computation.1 | async-start | bytes 7077888 | tf_op jit(solution)/shard_map/all_to_all | solution.py:25
  193.1 48.8 %copy-start.3 = (f32[256,1152]{1,0:T(8,128)S(1)}, f32[256,1152]{1,0:T(8,128)}, u32[]{:S(2)}) copy-start(f32[256,1152]{1,0:T(8,128)} %copy-done.2) | copy-start | bytes 3538948
  193.1 46.3 %collective-permute-start.3 = (bf16[256,1152]{1,0:T(8,128)(2,1)S(1)}, bf16[256,1152]{1,0:T(8,128)(2,1)S(1)}, u32[]{:S(2)}, u32[]{:S(2)}) collective-permute-start(bf16[256,1152]{1,0:T(8,128)(2,1)S(1)} %fusion.83), channel_id=1, source_target_pairs={{255,0},{0,1},{1,2},{2,3},{3,4},{4,5},{5,6},{6,7},{7,8},{8,9},{9,1... | collective-permute-start | bytes 1769480 | tf_op jit(solution)/shard_map/ppermute | solution.py:15
  239.5 9.3 %collective-permute-start.4 = (bf16[256,1152]{1,0:T(8,128)(2,1)S(1)}, bf16[256,1152]{1,0:T(8,128)(2,1)S(1)}, u32[]{:S(2)}, u32[]{:S(2)}) collective-permute-start(bf16[256,1152]{1,0:T(8,128)(2,1)S(1)} %collective-permute-done.3), channel_id=1, source_target_pairs={{255,0},{0,1},{1,2},{2,3},{3,4},{4,5},{5,6},{6,7},{7,8},{8,9},{9,1... | collective-permute-start | bytes 1769480 | tf_op jit(solution)/shard_map/ppermute | solution.py:15
  248.8 24.4 %collective-permute-start.5 = (bf16[256,1152]{1,0:T(8,128)(2,1)S(1)}, bf16[256,1152]{1,0:T(8,128)(2,1)}, u32[]{:S(2)}, u32[]{:S(2)}) collective-permute-start(bf16[256,1152]{1,0:T(8,128)(2,1)S(1)} %collective-permute-done.4), channel_id=1, source_target_pairs={{255,0},{0,1},{1,2},{2,3},{3,4},{4,5},{5,6},{6,7},{7,8},{8,9},{9,1... | collective-permute-start | bytes 1769480 | tf_op jit(solution)/shard_map/ppermute | solution.py:15
  261.4 30.0 %all-to-all-start.2 = ((bf16[32,6,1152]{2,1,0:T(8,128)(2,1)}), bf16[32,6,1152]{2,1,0:T(8,128)(2,1)S(1)}, u32[]{:S(2)}, u32[]{:S(2)}) async-start(bf16[32,6,1152]{2,1,0:T(8,128)(2,1)} %copy.15), calls=%async_computation.2 | async-start | bytes 1179648 | tf_op jit(solution)/shard_map/all_to_all | solution.py:33
